TPU v7x, 256 devices: a whole 4x4x8 slice. The times are simulated.
256 devices in a mesh: seq: 8 (over z), chan: 32 (over y, x, core).
Axes of the slice: x: 4, y: 4, z: 8, core: 2. Of those that a mesh axis runs over, the one named last changes fastest.
Arguments:
- tokens: bfloat16 [8192, 4096], P('seq', 'chan'), may hold values from -8 to 8
- norm_gain: float32 [4096], replicated, may hold values from 0.5 to 1.5
- gate_proj: bfloat16 [4096, 8192], P(None, 'chan'), may hold values from -0.09375 to 0.09375
- inner_proj: bfloat16 [4096, 8192], P(None, 'chan'), may hold values from -0.09375 to 0.09375
- state_proj: bfloat16 [4096, 384], P('chan'), may hold values from -0.11816406 to 0.11816406
- conv_inner: float32 [4, 8192], P(None, 'chan'), may hold values from -3 to 3
- conv_state: float32 [4, 256], replicated, may hold values from -3 to 3
- log_rate: float32 [128], P('chan'), may hold values from -1 to 0
- rate_bias: float32 [128], P('chan'), may hold values from -16 to -2
- skip_gain: float32 [128], P('chan'), may hold values from 0.2 to 4
- gate_gain: float32 [8192], P('chan'), may hold values from 0.5 to 1.5
- out_proj: bfloat16 [8192, 4096], P('chan'), may hold values from -0.125 to 0.125
Outputs:
- layer_out: bfloat16 [8192, 4096], P('seq', 'chan')
All inputs are finite; a program needn't handle non-finite values.
Results may differ from a plain program's by a relative error of at most 0.012.
Values may be sent and summed in bfloat16 or wider, within the bound.
A program may use at most 128 MiB of HBM per device.

v0:
```python
import jax
import jax.numpy as jnp
from jax import lax
from jax.sharding import PartitionSpec as P

P_SIZE = 64
N = 128
K = 4
Q = 256
DI = 8192


def from_behind(value, axis, steps):
    count = lax.axis_size(axis)
    leading, last = (max(0, -steps), min(count, count - steps))
    return lax.ppermute(value, axis, [(source, source + steps) for source in range(leading, last)])


def prefix(value, axis, join, neutral):
    count, mine = (lax.axis_size(axis), lax.axis_index(axis))
    pieces = jax.tree.map(lambda part: lax.all_gather(part, axis), value)
    total = jax.tree.map(
        lambda part, zero: jnp.full_like(part, 0) + jnp.asarray(zero, part.dtype), value, neutral
    )

    def turn(position, total):
        longer = join(total, jax.tree.map(lambda part: part[position], pieces))
        return jax.tree.map(lambda new, old: jnp.where(position < mine, new, old), longer, total)

    return lax.fori_loop(0, count - 1, turn, total)


def from_everyone(x, axis):
    size = lax.axis_size(axis)
    return lax.all_to_all(jnp.broadcast_to(x[None], (size, *x.shape)), axis, 0, 0, tiled=True)


def over_copies(x, axis):
    everything = from_everyone(x, axis)
    return jnp.sum(everything, axis=0)


def causal_mix(rim_part, fresh_rows, weights):
    length = fresh_rows.shape[0]
    padded = jnp.concatenate([rim_part.astype(jnp.float32), fresh_rows.astype(jnp.float32)], axis=0)
    summed = jnp.zeros(fresh_rows.shape, jnp.float32)
    for offset in range(weights.shape[0]):
        summed = summed + weights[offset] * padded[offset : offset + length]
    return jax.nn.silu(summed)


def combine_pair(earlier_part, later_part):
    return (
        earlier_part[0] * later_part[0],
        later_part[0][:, None, None] * earlier_part[1] + later_part[1],
    )


def local(
    tokens,
    norm_gain,
    gate_proj,
    inner_proj,
    state_proj,
    conv_inner,
    conv_state,
    log_rate,
    rate_bias,
    skip_gain,
    gate_gain,
    out_proj,
):
    gathered = lax.all_gather(tokens, "chan", axis=1, tiled=True)
    widened = gathered.astype(jnp.float32)
    inverse = lax.rsqrt(jnp.mean(widened * widened, axis=1, keepdims=True) + 1e-05)
    normed = (widened * inverse * norm_gain).astype(jnp.bfloat16)
    gate_raw = jnp.dot(normed, gate_proj, preferred_element_type=jnp.float32).astype(jnp.bfloat16)
    inner_raw = jnp.dot(normed, inner_proj, preferred_element_type=jnp.float32).astype(jnp.bfloat16)
    heads = log_rate.shape[0]
    start_head = lax.axis_index("chan") * heads
    projected = jnp.dot(
        normed,
        lax.all_gather(state_proj, "chan", axis=0, tiled=True),
        preferred_element_type=jnp.float32,
    )
    state_raw = projected[:, : 2 * N]
    raw_rate = lax.dynamic_slice_in_dim(projected, 2 * N + start_head, heads, 1)
    rim_rows = from_behind(
        (inner_raw[-(K - 1) :].astype(jnp.float32), state_raw[-(K - 1) :]), "seq", 1
    )
    inner_conv = causal_mix(rim_rows[0].astype(jnp.bfloat16), inner_raw, conv_inner)
    state_conv = causal_mix(rim_rows[1], state_raw, conv_state)
    token_rows = tokens.shape[0]
    blocks = token_rows // Q
    step_size = jax.nn.softplus(raw_rate + rate_bias)
    decay_log = -jnp.exp(log_rate) * step_size
    values = inner_conv.reshape(blocks, Q, heads, P_SIZE)
    in_map = state_conv[:, :N].reshape(blocks, Q, N)
    out_map = state_conv[:, N:].reshape(blocks, Q, N)
    step_rows = step_size.reshape(blocks, Q, heads).transpose(0, 2, 1)
    log_rows = decay_log.reshape(blocks, Q, heads).transpose(0, 2, 1)
    lower_mask = (jnp.arange(Q)[:, None] >= jnp.arange(Q)[None, :]).astype(jnp.float32)
    within = jnp.einsum("chs,ts->cht", log_rows, lower_mask)
    log_gaps = within[..., :, None] - within[..., None, :]
    fading = jnp.exp(jnp.where(lower_mask > 0, log_gaps, -jnp.inf))
    scores = jnp.einsum("ctn,csn->cts", out_map, in_map)
    mixing = scores[:, None] * fading * step_rows[:, :, None, :]
    local_out = jnp.einsum("chts,cshp->cthp", mixing, values)
    tail_weight = jnp.exp(within[..., -1:] - within) * step_rows
    scaled = values * tail_weight.transpose(0, 2, 1)[..., None]
    block_end = jnp.einsum("csn,cshp->chnp", in_map, scaled)
    block_log = within[..., -1]
    through = jnp.cumsum(block_log, axis=0)
    before = through - block_log
    earlier = jnp.arange(blocks)[:, None] > jnp.arange(blocks)[None, :]
    passage = jnp.exp(
        jnp.where(earlier[:, :, None], before[:, None, :] - through[None, :, :], -jnp.inf)
    )
    entering = jnp.einsum("cdh,dhnp->chnp", passage, block_end)
    device_end = jnp.einsum("ch,chnp->hnp", jnp.exp(through[-1:] - through), block_end)
    device_fade = jnp.exp(through[-1])
    identity = (jnp.ones_like(device_fade), jnp.zeros_like(device_end))
    carried = prefix((device_fade, device_end), "seq", combine_pair, identity)[1]
    entering = entering + jnp.exp(before)[:, :, None, None] * carried[None]
    carried_out = jnp.einsum("ctn,chnp->cthp", out_map, entering)
    carried_out = carried_out * jnp.exp(within).transpose(0, 2, 1)[..., None]
    skip_wide = jnp.repeat(skip_gain, P_SIZE)
    ssd_out = (local_out + carried_out).reshape(token_rows, heads * P_SIZE) + skip_wide * inner_conv
    gated_out = ssd_out * jax.nn.silu(gate_raw.astype(jnp.float32))
    energy = over_copies(jnp.sum(gated_out * gated_out, axis=1), "chan")
    norm_scale = lax.rsqrt(energy / DI + 1e-05)
    shaped = (gated_out * norm_scale[:, None] * gate_gain).astype(jnp.bfloat16)
    column_rows = lax.all_to_all(out_proj, "chan", split_axis=1, concat_axis=0, tiled=True)
    summed = jnp.dot(
        lax.all_gather(shaped, "chan", axis=1, tiled=True),
        column_rows,
        preferred_element_type=jnp.float32,
    )
    return (tokens.astype(jnp.float32) + summed).astype(jnp.bfloat16)


def solution(mesh):
    return jax.shard_map(
        local,
        mesh=mesh,
        in_specs=(
            P("seq", "chan"),
            P(),
            P(None, "chan"),
            P(None, "chan"),
            P("chan", None),
            P(None, "chan"),
            P(),
            P("chan"),
            P("chan"),
            P("chan"),
            P("chan"),
            P("chan", None),
        ),
        out_specs=P("seq", "chan"),
        check_vma=False,
    )
```

profile of v0, /device:TPU:1, one launch (start us, length us, event | category | flops | bytes accessed | tf_op | source)
XLA Modules:
  0.0 364.0 jit_solution(8693260345117643009)
XLA Ops:
  6.5 0.7 all-gather.7.cloned.1.call-update
  7.3 0.7 all-gather.9.cloned.1.call-update
  8.1 0.7 exponential_negate_fusion
  8.7 0.8 fusion.68
  9.6 0.8 fusion.69
  10.4 67.4 %all-gather.7.cloned.1.call-done = bf16[1024,4096]{1,0:T(8,128)(2,1)} async-done(((bf16[1024,128]{1,0:T(8,128)(2,1)}), bf16[1024,4096]{1,0:T(8,128)(2,1)}) %all-gather.7.cloned.1.call-update) | async-done | bytes 8388624 | tf_op jit(solution)/shard_map/all_gather | solution.py:73
  77.8 5.1 %fusion.1 = f32[1024]{0:T(1024)S(1)} fusion(bf16[1024,4096]{1,0:T(8,128)(2,1)} %all-gather.7.cloned.1.call-done), kind=kLoop, calls=%fused_computation.6 | loop fusion | flops 12581888 | bytes 8392704 | tf_op jit(solution)/shard_map/reduce_sum | solution.py:75
  82.9 47.1 %all-gather.9.cloned.1.call-done = bf16[4096,384]{1,0:T(8,128)(2,1)} async-done(((bf16[128,384]{1,0:T(8,128)(2,1)}), bf16[4096,384]{1,0:T(8,128)(2,1)}) %all-gather.9.cloned.1.call-update) | async-done | bytes 3145744 | tf_op jit(solution)/shard_map/all_gather | solution.py:83
  130.0 8.1 %fusion.63 = f32[1024,384]{1,0:T(8,128)S(1)} fusion(bf16[4096,384]{1,0:T(8,128)(2,1)} %all-gather.9.cloned.1.call-done, bf16[1024,4096]{1,0:T(8,128)(2,1)} %all-gather.7.cloned.1.call-done, f32[4096]{0:T(1024)S(1)} %copy-done.10, f32[1024]{0:T(1024)S(1)} %add_rsqrt_fusion.1), kind=kOutput, calls=%fused_computation.97 | convolution fusion | flops 3238002688 | bytes 13127680 | tf_op jit(solution)/shard_map/dot_general | solution.py:81
  138.1 3.2 collective-permute-start.1
  141.3 0.2 constant_dynamic-slice_fusion.1
  141.5 0.2 copy.156
  141.8 0.2 fusion.50
  142.0 0.2 slice_reduce_fusion
  142.3 5.9 %fusion.70 = (f32[1024,256]{1,0:T(8,128)S(1)}, bf16[1024,256]{1,0:T(8,128)(2,1)S(1)}) fusion(bf16[4096,256]{1,0:T(8,128)(2,1)S(1)} %copy-done, bf16[1024,4096]{1,0:T(8,128)(2,1)} %all-gather.7.cloned.1.call-done, f32[4096]{0:T(1024)S(1)} %copy-done.10, f32[1024]{0:T(1024)S(1)} %add_rsqrt_fusion.1), kind=kOutput, calls=%fused_computation.102 | convolution fusion | flops 2164785152 | bytes 12079104 | tf_op jit(solution)/shard_map/dot_general | solution.py:78
  148.2 3.2 collective-permute-start
  151.5 1.1 slice.93
  152.6 0.6 divide_multiply_fusion.1
  153.2 1.3 copy.120
  154.5 2.8 reshape.81
  157.3 1.4 broadcast_multiply_fusion
  158.7 3.1 divide_multiply_fusion
  161.9 0.7 copy-done.5
  162.6 0.9 fusion.47
  164.2 12.4 %all-gather.1 = f32[8,1,4]{2,1,0:T(1,128)S(1)} all-gather(f32[1,1,4]{2,1,0:T(1,128)S(1)} %get-tuple-element.179), channel_id=1, replica_groups=mesh['seq'=8,'chan'=32] {'seq'}, dimensions={0}, use_global_device_ids=true | all-gather | bytes 144 | tf_op jit(solution)/shard_map/all_gather | solution.py:21
  176.6 2.2 fusion.71
  178.8 19.2 %all-gather.13.cloned.1.call-done = f32[32,128,64]{1,2,0:T(8,128)} async-done(((f32[4,128,64]{1,2,0:T(8,128)}), f32[32,128,64]{1,2,0:T(8,128)}) %all-gather.13.cloned.1.call-update) | async-done | bytes 1048592 | tf_op jit(solution)/shard_map/all_gather | solution.py:21
  198.0 8.4 %while.14 = (s32[]{:T(128)}, f32[4,128,64]{2,1,0:T(8,128)S(1)}, s32[]{:T(128)}, f32[8,4]{1,0:T(8,128)S(1)}, f32[8,4,128,64]{2,3,1,0:T(8,128)}, /*index=5*/s32[]{:T(128)}, s32[]{:T(128)}) while((s32[]{:T(128)}, f32[4,128,64]{2,1,0:T(8,128)S(1)}, s32[]{:T(128)}, f32[8,4]{1,0:T(8,128)S(1)}, f32[8,4,128,64]{2,3,1,0:T(8,128)}, ...), condition=%wide.region_3.4_spmd.clone, body=%wide.region_2.3_spmd.clone.sunk | while | flops 131076 | bytes 917665 | solution.py:30
  198.0 0.9 constant_dynamic-slice_fusion.3
  199.2 0.9 constant_dynamic-slice_fusion.3
  200.4 0.9 constant_dynamic-slice_fusion.3
  201.6 0.9 constant_dynamic-slice_fusion.3
  202.8 0.9 constant_dynamic-slice_fusion.3
  204.0 0.9 constant_dynamic-slice_fusion.3
  205.2 0.9 constant_dynamic-slice_fusion.3
  206.5 0.4 fusion.22
  206.9 0.3 fusion.72
  207.2 3.9 %fusion.19 = f32[4,256,4,64]{1,3,2,0:T(8,128)} fusion(f32[4,4,256]{2,1,0:T(4,128)S(1)} %copy.123, f32[4,4,256]{2,1,0:T(4,128)S(1)} %fusion.50, f32[4,256,256]{2,1,0:T(8,128)} %fusion.71, pred[256,256]{1,0:T(8,128)(4,1)S(1)} %convert_compare_fusion, f32[4,256,4,64]{1,0,3,2:T(4,128)} %reshape.81, f32[4,256,4,64]{1,3,2,0:T(8,128)S(1)} %bitcast.90, ...), kind=kOutput, calls=%fused_computation.26 | convolution fusion | flops 138936320 | bytes 4308992 | tf_op jit(solution)/shard_map/chts,cshp->cthp/dot_general | solution.py:108
  211.1 2.9 copy.152
  213.9 3.2 reshape.97
  217.2 7.8 %multiply_reduce_fusion = (f32[1024]{0:T(1024)S(1)}, f32[1024,256]{1,0:T(8,128)}) fusion(bf16[4096,256]{1,0:T(8,128)(2,1)} %param.16, bf16[1024,4096]{1,0:T(8,128)(2,1)} %all-gather.7.cloned.1.call-done, f32[4096]{0:T(1024)S(1)} %copy-done.10, f32[1024]{0:T(1024)S(1)} %add_rsqrt_fusion.1, f32[1024,256]{1,0:T(8,128)} %reshape.97, ...), kind=kOutput, calls=%fused_computation.61 | convolution fusion | flops 2167143424 | bytes 13657088 | tf_op jit(solution)/shard_map/dot_general | solution.py:77
  225.0 19.9 %all_to_all.25 = f32[32,1,1024]{2,1,0:T(1,128)S(1)} all-to-all(f32[32,1,1024]{2,1,0:T(1,128)S(1)} %broadcast_in_dim.32), channel_id=1, replica_groups=mesh['seq'=8,'chan'=32] {'chan'}, dimensions={0} | all-to-all | bytes 262144 | tf_op jit(solution)/shard_map/all_to_all | solution.py:35
  245.1 2.2 multiply_convert_fusion
  247.4 4.1 %copy.141 = bf16[256,4096]{0,1:T(8,128)(2,1)} copy(bf16[256,4096]{1,0:T(8,128)(2,1)} %param.25) | data formatting | bytes 4194304 | tf_op args[11]
  251.4 39.8 %all_to_all.26 = bf16[256,32,128]{0,2,1:T(8,128)(2,1)} all-to-all(bf16[256,32,128]{0,2,1:T(8,128)(2,1)} %bitcast.86), channel_id=1, replica_groups=mesh['seq'=8,'chan'=32] {'chan'}, dimensions={1} | all-to-all | bytes 4194304 | tf_op jit(solution)/shard_map/all_to_all | solution.py:133
  291.3 4.1 %copy.142 = bf16[32,256,128]{2,1,0:T(8,128)(2,1)} copy(bf16[32,256,128]{1,2,0:T(8,128)(2,1)} %bitcast.85) | data formatting | bytes 4194304 | tf_op jit(solution)/shard_map/all_to_all | solution.py:133
  295.3 50.5 %all-gather.11.cloned.1.call-done = bf16[1024,8192]{1,0:T(8,128)(2,1)} async-done(((bf16[1024,256]{1,0:T(8,128)(2,1)}), bf16[1024,8192]{1,0:T(8,128)(2,1)}) %all-gather.11.cloned.1.call-update) | async-done | bytes 16777232 | tf_op jit(solution)/shard_map/all_gather | solution.py:135
  345.8 11.6 %fusion.23 = bf16[1024,128]{1,0:T(8,128)(2,1)} fusion(bf16[1024,8192]{1,0:T(8,128)(2,1)} %all-gather.11.cloned.1.call-done, bf16[8192,128]{1,0:T(8,128)(2,1)} %bitcast.89, bf16[1024,128]{1,0:T(8,128)(2,1)S(1)} %copy-done.6), kind=kOutput, calls=%fused_computation.34 | convolution fusion | flops 2147876864 | bytes 19398656 | tf_op jit(solution)/shard_map/dot_general | solution.py:134
  (77 shorter events, 3.0 us)
Async XLA Ops:
  6.5 135.8 %copy-start = (bf16[4096,256]{1,0:T(8,128)(2,1)S(1)}, bf16[4096,256]{1,0:T(8,128)(2,1)}, u32[]{:S(2)}) copy-start(bf16[4096,256]{1,0:T(8,128)(2,1)} %param.17) | copy-start | bytes 6291460
  6.5 71.3 %all-gather.7.cloned.1.call-start = ((), (), s32[]{:S(2)}) async-start(), calls=%async_computation.2 | async-start | bytes 8650752 | tf_op jit(solution)/shard_map/all_gather | solution.py:73
  7.3 122.7 %all-gather.9.cloned.1.call-start = ((), (), s32[]{:S(2)}) async-start(), calls=%async_computation.3 | async-start | bytes 3244032 | tf_op jit(solution)/shard_map/all_gather | solution.py:83
  8.0 189.9 %all-gather.13.cloned.1.call-start = ((), (), s32[]{:S(2)}) async-start(), calls=%async_computation.5 | async-start | bytes 1179648 | tf_op jit(solution)/shard_map/all_gather | solution.py:21
  10.4 119.6 %copy-start.10 = (f32[4096]{0:T(1024)S(1)}, f32[4096]{0:T(1024)}, u32[]{:S(2)}) copy-start(f32[4096]{0:T(1024)} %param.15) | copy-start | bytes 49156
  82.9 58.8 %copy-start.8 = (f32[4]{0:T(128)S(1)}, f32[4]{0:T(128)}, u32[]{:S(2)}) copy-start(f32[4]{0:T(128)} %param.22) | copy-start | bytes 52
  138.1 3.2 copy-start.3
  138.1 20.6 %collective-permute-start.1 = (f32[3,256]{1,0:T(4,128)S(1)}, f32[3,256]{1,0:T(4,128)S(1)}, u32[]{:S(2)}, u32[]{:S(2)}) collective-permute-start(f32[3,256]{1,0:T(4,128)S(1)} %slice.92), channel_id=1, source_target_pairs={{0,32},{32,64},{64,96},{96,128},{128,160},{160,192},{192,224},{1,3... | collective-permute-start | bytes 9224 | tf_op jit(solution)/shard_map/ppermute | solution.py:16
  142.3 9.1 %copy-start.4 = (f32[1024,384]{1,0:T(8,128)S(1)}, f32[1024,384]{1,0:T(8,128)}, u32[]{:S(2)}) copy-start(f32[1024,384]{1,0:T(8,128)} %copy-done.3) | copy-start | bytes 4718596
  148.2 4.3 %collective-permute-start = (bf16[3,256]{1,0:T(4,128)(2,1)S(1)}, bf16[3,256]{1,0:T(4,128)(2,1)S(1)}, u32[]{:S(2)}, u32[]{:S(2)}) collective-permute-start(bf16[3,256]{1,0:T(4,128)(2,1)S(1)} %slice.161), channel_id=1, source_target_pairs={{0,32},{32,64},{64,96},{96,128},{128,160},{160,192},{192,224},{1,3... | collective-permute-start | bytes 4616 | tf_op jit(solution)/shard_map/ppermute | solution.py:16
  153.2 8.7 %copy-start.1 = (f32[1024,256]{1,0:T(8,128)}, f32[1024,256]{1,0:T(8,128)S(1)}, u32[]{:S(2)}) copy-start(f32[1024,256]{1,0:T(8,128)S(1)} %divide_multiply_fusion.1) | copy-start | bytes 3145732
  154.5 9.1 %copy-start.9 = (f32[4]{0:T(128)S(1)}, f32[4]{0:T(128)}, u32[]{:S(2)}) copy-start(f32[4]{0:T(128)} %param.23) | copy-start | bytes 52
  161.9 0.7 copy-start.5
  163.6 182.2 %all-gather.11.cloned.1.call-start = ((), (), s32[]{:S(2)}) async-start(), calls=%async_computation.4 | async-start | bytes 17301504 | tf_op jit(solution)/shard_map/all_gather | solution.py:135
  211.1 6.1 %copy-start.2 = (f32[1024,256]{1,0:T(8,128)S(1)}, f32[1024,256]{1,0:T(8,128)}, u32[]{:S(2)}) copy-start(f32[1024,256]{1,0:T(8,128)} %copy-done.1) | copy-start | bytes 3145732
  217.2 27.9 %copy-start.7 = (f32[256]{0:T(256)S(1)}, f32[256]{0:T(256)}, u32[]{:S(2)}) copy-start(f32[256]{0:T(256)} %param.24) | copy-start | bytes 3076
  251.4 94.4 %copy-start.6 = (bf16[1024,128]{1,0:T(8,128)(2,1)S(1)}, bf16[1024,128]{1,0:T(8,128)(2,1)}, u32[]{:S(2)}) copy-start(bf16[1024,128]{1,0:T(8,128)(2,1)} %param.14) | copy-start | bytes 786436
Sparse Core Ops, SparseCore 0:
  9.8 67.9 all-gather.6
  80.4 49.5 all-gather.8
  163.7 34.1 all-gather.12
  247.5 98.2 all-gather.10
where the time goes:
time: 365 us; the launch traced here: 364 us
  waiting for transfers between devices  186 us (51%)
  blocking collectives  72.1 us (20%)
  matrix products  41.3 us (11%)
  local copies, waits for them, and re-layouts  30.5 us (8%)
  other arithmetic  14.3 us (4%)
  between operations  13.4 us (4%)
  starting transfers between devices  6.52 us (2%)
    all_gather x1, waiting for transfers between devices, local(): gathered = lax.all_gather(tokens, 'chan', axis=1, tiled=True)  67.4 us
    all_gather x1, waiting for transfers between devices, local(): lax.all_gather(shaped, 'chan', axis=1, tiled=True)  50.5 us
    all_gather x1, waiting for transfers between devices, local(): lax.all_gather(state_proj, 'chan', axis=0, tiled=True)  47.1 us
    all_to_all x1, blocking collectives, local(): lax.all_to_all(out_proj, 'chan', split_axis=1, concat_axis=0, tiled=True)  39.8 us
    all_to_all x1, blocking collectives, from_everyone(): lax.all_to_all(jnp.broadcast_to(x[None], (size, *x.shape)), axis, 0, 0, t...  19.9 us
    all_gather x1, waiting for transfers between devices, prefix(): pieces = jax.tree.map(lambda part: lax.all_gather(part, axis), value)  19.2 us
    all_gather x1, blocking collectives, prefix(): pieces = jax.tree.map(lambda part: lax.all_gather(part, axis), value)  12.4 us
    dot_general x1, matrix products, local(): jnp.dot(lax.all_gather(shaped, 'chan', axis=1, tiled=True), column_rows,...  11.6 us
  transfers between devices with their start and end apart: 6, of which 4 were waited for; matrix products, arithmetic and copies ran while one was open for 9% of the time, Pallas kernels for 0%

commit v1 on v0

--- a/solution.py
+++ b/solution.py
@@ -70,7 +70,9 @@
     gate_gain,
     out_proj,
 ):
-    gathered = lax.all_gather(tokens, "chan", axis=1, tiled=True)
+    gathered = jnp.concatenate(
+        lax.all_to_all(jnp.stack([tokens] * lax.axis_size("chan")), "chan", 0, 0), axis=1
+    )
     widened = gathered.astype(jnp.float32)
     inverse = lax.rsqrt(jnp.mean(widened * widened, axis=1, keepdims=True) + 1e-05)
     normed = (widened * inverse * norm_gain).astype(jnp.bfloat16)

time: 365 us -> 369 us (1.011)
  starting transfers between devices: 6.52 us -> 15.1 us
  waiting for transfers between devices: 186 us -> 180 us
    all_to_all x0 -> x1, waiting for transfers between devices: none -> 105 us  [local(): lax.all_to_all(jnp.stack([tokens] * lax.axis_size('chan')), 'chan', 0, 0)]
    all_gather x1 -> x0, waiting for transfers between devices: 67.4 us -> none  [local(): gathered = lax.all_gather(tokens, 'chan', axis=1, tiled=True)]
    all_gather x1, waiting for transfers between devices: 47.1 us -> 0.01 us  [local(): lax.all_gather(state_proj, 'chan', axis=0, tiled=True)]
    all_to_all x0 -> x1, starting transfers between devices: none -> 8.77 us  [local(): lax.all_to_all(jnp.stack([tokens] * lax.axis_size('chan')), 'chan', 0, 0)]
    convert_element_type x0 -> x1, other arithmetic: none -> 7.75 us  [local(): normed = (widened * inverse * norm_gain).astype(jnp.bfloat16)]
    another operation x0 -> x1, local copies, waits for them, and re-layouts: none -> 4.32 us  [local(): jnp.stack([tokens] * lax.axis_size('chan'))]
  transfers between devices with their start and end apart: 6 -> 6, of which waited for: 4 -> 3; matrix products, arithmetic and copies ran while one was open for 9% -> 6% of each run, Pallas kernels for 0% -> 0%
where the time goes in v1:
time: 369 us; the launch traced here: 368 us
  waiting for transfers between devices  180 us (49%)
  blocking collectives  75.3 us (20%)
  matrix products  37.9 us (10%)
  local copies, waits for them, and re-layouts  28.8 us (8%)
  other arithmetic  17.7 us (5%)
  starting transfers between devices  15.1 us (4%)
  between operations  13.5 us (4%)
    all_to_all x1, waiting for transfers between devices, local(): lax.all_to_all(jnp.stack([tokens] * lax.axis_size('chan')), 'chan', 0, 0)  105 us
    all_gather x1, waiting for transfers between devices, local(): lax.all_gather(shaped, 'chan', axis=1, tiled=True)  50.8 us
    all_to_all x1, blocking collectives, local(): lax.all_to_all(out_proj, 'chan', split_axis=1, concat_axis=0, tiled=True)  41 us
    all_gather x1, waiting for transfers between devices, prefix(): pieces = jax.tree.map(lambda part: lax.all_gather(part, axis), value)  22.5 us
    all_to_all x1, blocking collectives, from_everyone(): lax.all_to_all(jnp.broadcast_to(x[None], (size, *x.shape)), axis, 0, 0, t...  20 us
    all_gather x1, blocking collectives, prefix(): pieces = jax.tree.map(lambda part: lax.all_gather(part, axis), value)  14.3 us
    dot_general x1, matrix products, local(): jnp.dot(lax.all_gather(shaped, 'chan', axis=1, tiled=True), column_rows,...  11.8 us
    all_to_all x1, starting transfers between devices, local(): lax.all_to_all(jnp.stack([tokens] * lax.axis_size('chan')), 'chan', 0, 0)  8.77 us
  transfers between devices with their start and end apart: 6, of which 3 were waited for; matrix products, arithmetic and copies ran while one was open for 6% of the time, Pallas kernels for 0%

profile of v1, /device:TPU:1, one launch (start us, length us, event | category | flops | bytes accessed | tf_op | source)
XLA Modules:
  0.0 367.9 jit_solution(14272128732492435278)
XLA Ops:
  6.5 1.2 copy.125
  7.8 4.3 %stack.2 = bf16[32,1024,128]{1,2,0:T(8,128)(2,1)} broadcast(bf16[1024,128]{0,1:T(8,128)(2,1)S(1)} %copy.125), dimensions={1,2} | broadcast | bytes 8650752 | tf_op jit(solution)/shard_map/stack | solution.py:74
  12.1 8.8 %all-to-all-start = ((bf16[32,1024,128]{1,2,0:T(8,128)(2,1)}), bf16[32,1024,128]{1,2,0:T(8,128)(2,1)}, u32[]{:S(2)}, u32[]{:S(2)}) async-start(bf16[32,1024,128]{1,2,0:T(8,128)(2,1)} %stack.2), calls=%async_computation | async-start | bytes 16777216 | tf_op jit(solution)/shard_map/all_to_all | solution.py:74
  20.9 0.7 all-gather.6.cloned.1.call-update
  21.7 105.4 %all-to-all-done = bf16[32,1024,128]{1,2,0:T(8,128)(2,1)} async-done(((bf16[32,1024,128]{1,2,0:T(8,128)(2,1)}), bf16[32,1024,128]{1,2,0:T(8,128)(2,1)}, u32[]{:S(2)}, u32[]{:S(2)}) %all-to-all-start) | async-done | bytes 8388640 | tf_op jit(solution)/shard_map/all_to_all | solution.py:74
  127.2 5.1 %multiply_reduce_fusion = f32[1024]{0:T(1024)S(1)} fusion(bf16[32,1024,128]{1,2,0:T(8,128)(2,1)} %all-to-all-done), kind=kLoop, calls=%fused_computation.7 | loop fusion | flops 12581888 | bytes 8392704 | tf_op jit(solution)/shard_map/reduce_sum | solution.py:77
  132.3 7.7 %fusion.2 = bf16[1024,4096]{0,1:T(8,128)(2,1)} fusion(f32[4096]{0:T(1024)S(1)} %copy-done.7, f32[1024]{0:T(1024)S(1)} %add_rsqrt_fusion.1, bf16[32,1024,128]{1,2,0:T(8,128)(2,1)} %all-to-all-done), kind=kLoop, calls=%fused_computation.6 | loop fusion | flops 16777216 | bytes 16797696 | tf_op jit(solution)/shard_map/convert_element_type | solution.py:78
  140.1 7.9 %fusion.66 = f32[1024,384]{1,0:T(8,128)S(1)} fusion(bf16[1024,4096]{0,1:T(8,128)(2,1)} %fusion.2, bf16[4096,384]{1,0:T(8,128)(2,1)} %all-gather.6.cloned.1.call-done), kind=kOutput, calls=%fused_computation.101 | convolution fusion | flops 3221225472 | bytes 13107200 | tf_op jit(solution)/shard_map/dot_general | solution.py:83
  148.0 1.2 copy-done.2
  149.2 0.2 constant_dynamic-slice_fusion.1
  149.4 0.2 copy.162
  149.7 0.2 fusion.49
  149.9 0.2 slice_reduce_fusion
  150.0 5.8 %fusion.65 = (f32[1024,256]{1,0:T(8,128)S(1)}, bf16[1024,256]{1,0:T(8,128)(2,1)S(1)}) fusion(bf16[1024,4096]{0,1:T(8,128)(2,1)} %fusion.2, bf16[4096,256]{1,0:T(8,128)(2,1)S(1)} %copy-done), kind=kOutput, calls=%fused_computation.100 | convolution fusion | flops 2148007936 | bytes 12058624 | tf_op jit(solution)/shard_map/dot_general | solution.py:80
  155.8 2.9 collective-permute-start
  158.9 0.8 slice.92
  159.7 3.3 collective-permute-start.1
  163.0 0.6 divide_multiply_fusion.1
  163.7 1.3 copy.126
  165.0 1.7 reshape.87
  166.7 0.2 broadcast_multiply_fusion
  166.9 0.6 divide_multiply_fusion
  167.6 0.9 fusion.46
  169.2 14.3 %all-gather.1 = f32[8,1,4]{2,1,0:T(1,128)S(1)} all-gather(f32[1,1,4]{2,1,0:T(1,128)S(1)} %get-tuple-element.179), channel_id=1, replica_groups=mesh['seq'=8,'chan'=32] {'seq'}, dimensions={0}, use_global_device_ids=true | all-gather | bytes 144 | tf_op jit(solution)/shard_map/all_gather | solution.py:21
  183.4 0.3 fusion.67
  183.7 22.5 %all-gather.10.cloned.1.call-done = f32[32,128,64]{1,2,0:T(8,128)} async-done(((f32[4,128,64]{1,2,0:T(8,128)}), f32[32,128,64]{1,2,0:T(8,128)}) %all-gather.10.cloned.1.call-update) | async-done | bytes 1048592 | tf_op jit(solution)/shard_map/all_gather | solution.py:21
  206.3 8.4 %while.14 = (s32[]{:T(128)}, f32[4,128,64]{2,1,0:T(8,128)S(1)}, s32[]{:T(128)}, f32[8,4]{1,0:T(8,128)S(1)}, f32[8,4,128,64]{2,3,1,0:T(8,128)}, /*index=5*/s32[]{:T(128)}, s32[]{:T(128)}) while((s32[]{:T(128)}, f32[4,128,64]{2,1,0:T(8,128)S(1)}, s32[]{:T(128)}, f32[8,4]{1,0:T(8,128)S(1)}, f32[8,4,128,64]{2,3,1,0:T(8,128)}, ...), condition=%wide.region_3.4_spmd.clone, body=%wide.region_2.3_spmd.clone.sunk | while | flops 131076 | bytes 917657 | solution.py:30
  206.3 0.9 constant_dynamic-slice_fusion.3
  207.5 0.9 constant_dynamic-slice_fusion.3
  208.7 0.9 constant_dynamic-slice_fusion.3
  209.6 0.1 copy.172
  209.9 0.9 constant_dynamic-slice_fusion.3
  211.1 0.9 constant_dynamic-slice_fusion.3
  212.3 0.9 constant_dynamic-slice_fusion.3
  213.5 0.9 constant_dynamic-slice_fusion.3
  214.8 0.4 fusion.21
  215.2 0.3 fusion.68
  215.5 2.4 fusion.18
  217.9 1.9 copy.158
  219.8 2.2 reshape.104
  222.0 8.0 %multiply_reduce_fusion.1 = (f32[1024]{0:T(1024)S(1)}, f32[1024,256]{1,0:T(8,128)}) fusion(bf16[1024,4096]{0,1:T(8,128)(2,1)} %fusion.2, bf16[4096,256]{1,0:T(8,128)(2,1)} %param.16, f32[1024,256]{1,0:T(8,128)} %reshape.104, f32[1024,256]{1,0:T(8,128)S(1)} %copy-done.4, f32[256]{0:T(256)S(1)} %mul.273), kind=kOutput, calls=%fused_computation.60 | convolution fusion | flops 2150366208 | bytes 13636608 | tf_op jit(solution)/shard_map/dot_general | solution.py:79
  230.1 20.0 %all_to_all.30 = f32[32,1,1024]{2,1,0:T(1,128)S(1)} all-to-all(f32[32,1,1024]{2,1,0:T(1,128)S(1)} %broadcast_in_dim.32), channel_id=1, replica_groups=mesh['seq'=8,'chan'=32] {'chan'}, dimensions={0} | all-to-all | bytes 262144 | tf_op jit(solution)/shard_map/all_to_all | solution.py:35
  250.2 2.2 multiply_convert_fusion
  252.4 2.5 copy.147
  254.9 41.0 %all_to_all.31 = bf16[256,32,128]{0,2,1:T(8,128)(2,1)S(1)} all-to-all(bf16[256,32,128]{0,2,1:T(8,128)(2,1)} %bitcast.97), channel_id=1, replica_groups=mesh['seq'=8,'chan'=32] {'chan'}, dimensions={1} | all-to-all | bytes 4194304 | tf_op jit(solution)/shard_map/all_to_all | solution.py:135
  295.9 2.9 copy.148
  298.8 50.8 %all-gather.8.cloned.1.call-done = bf16[1024,8192]{1,0:T(8,128)(2,1)} async-done(((bf16[1024,256]{1,0:T(8,128)(2,1)}), bf16[1024,8192]{1,0:T(8,128)(2,1)}) %all-gather.8.cloned.1.call-update) | async-done | bytes 16777232 | tf_op jit(solution)/shard_map/all_gather | solution.py:137
  349.7 11.8 %fusion.22 = bf16[1024,128]{1,0:T(8,128)(2,1)} fusion(bf16[1024,8192]{1,0:T(8,128)(2,1)} %all-gather.8.cloned.1.call-done, bf16[8192,128]{1,0:T(8,128)(2,1)} %bitcast.100, bf16[1024,128]{1,0:T(8,128)(2,1)S(1)} %copy-done.6), kind=kOutput, calls=%fused_computation.33 | convolution fusion | flops 2147876864 | bytes 19398656 | tf_op jit(solution)/shard_map/dot_general | solution.py:136
  (86 shorter events, 2.9 us)
Async XLA Ops:
  6.5 143.5 %copy-start = (bf16[4096,256]{1,0:T(8,128)(2,1)S(1)}, bf16[4096,256]{1,0:T(8,128)(2,1)}, u32[]{:S(2)}) copy-start(bf16[4096,256]{1,0:T(8,128)(2,1)} %param.17) | copy-start | bytes 6291460
  12.1 9.6 %copy-start.13 = (f32[4]{0:T(128)S(1)}, f32[4]{0:T(128)}, u32[]{:S(2)}) copy-start(f32[4]{0:T(128)} %param.21) | copy-start | bytes 52
  12.1 9.6 %copy-start.8 = (f32[4,256]{1,0:T(4,128)S(1)}, f32[4,256]{1,0:T(4,128)}, u32[]{:S(2)}) copy-start(f32[4,256]{1,0:T(4,128)} %param.19) | copy-start | bytes 12292
  12.1 9.6 %copy-start.9 = (f32[4,256]{1,0:T(4,128)S(1)}, f32[4,256]{1,0:T(4,128)}, u32[]{:S(2)}) copy-start(f32[4,256]{1,0:T(4,128)} %param.20) | copy-start | bytes 12292
  12.1 115.1 %all-to-all-start = ((bf16[32,1024,128]{1,2,0:T(8,128)(2,1)}), bf16[32,1024,128]{1,2,0:T(8,128)(2,1)}, u32[]{:S(2)}, u32[]{:S(2)}) async-start(bf16[32,1024,128]{1,2,0:T(8,128)(2,1)} %stack.2), calls=%async_computation | async-start | bytes 16777216 | tf_op jit(solution)/shard_map/all_to_all | solution.py:74
  20.9 119.2 %all-gather.6.cloned.1.call-start = ((), (), s32[]{:S(2)}) async-start(), calls=%async_computation.3 | async-start | bytes 3244032 | tf_op jit(solution)/shard_map/all_gather | solution.py:85
  21.6 184.7 %all-gather.10.cloned.1.call-start = ((), (), s32[]{:S(2)}) async-start(), calls=%async_computation.5 | async-start | bytes 1179648 | tf_op jit(solution)/shard_map/all_gather | solution.py:21
  21.7 110.6 %copy-start.7 = (f32[4096]{0:T(1024)S(1)}, f32[4096]{0:T(1024)}, u32[]{:S(2)}) copy-start(f32[4096]{0:T(1024)} %param.15) | copy-start | bytes 49156
  140.1 9.5 %copy-start.11 = (f32[4]{0:T(128)S(1)}, f32[4]{0:T(128)}, u32[]{:S(2)}) copy-start(f32[4]{0:T(128)} %param.22) | copy-start | bytes 52
  148.0 1.2 copy-start.2
  155.8 7.2 %collective-permute-start = (bf16[3,256]{1,0:T(4,128)(2,1)S(1)}, bf16[3,256]{1,0:T(4,128)(2,1)S(1)}, u32[]{:S(2)}, u32[]{:S(2)}) collective-permute-start(bf16[3,256]{1,0:T(4,128)(2,1)S(1)} %slice.161), channel_id=1, source_target_pairs={{0,32},{32,64},{64,96},{96,128},{128,160},{160,192},{192,224},{1,3... | collective-permute-start | bytes 4616 | tf_op jit(solution)/shard_map/ppermute | solution.py:16
  158.9 8.0 %slice-start = ((f32[1024,384]{1,0:T(8,128)}), f32[1024,256]{1,0:T(8,128)S(1)}, s32[]{:S(2)}) async-start(f32[1024,384]{1,0:T(8,128)} %copy-done.2), calls=%async_computation.6 | async-start | bytes 2097152 | tf_op jit(solution)/shard_map/slice | solution.py:88
  159.7 7.2 %collective-permute-start.1 = (f32[3,256]{1,0:T(4,128)S(1)}, f32[3,256]{1,0:T(4,128)S(1)}, u32[]{:S(2)}, u32[]{:S(2)}) collective-permute-start(f32[3,256]{1,0:T(4,128)S(1)} %slice.92), channel_id=1, source_target_pairs={{0,32},{32,64},{64,96},{96,128},{128,160},{160,192},{192,224},{1,3... | collective-permute-start | bytes 9224 | tf_op jit(solution)/shard_map/ppermute | solution.py:16
  163.7 3.9 %copy-start.3 = (f32[1024,256]{1,0:T(8,128)}, f32[1024,256]{1,0:T(8,128)S(1)}, u32[]{:S(2)}) copy-start(f32[1024,256]{1,0:T(8,128)S(1)} %divide_multiply_fusion.1) | copy-start | bytes 3145732
  165.0 3.7 copy-start.12
  168.6 181.1 %all-gather.8.cloned.1.call-start = ((), (), s32[]{:S(2)}) async-start(), calls=%async_computation.4 | async-start | bytes 17301504 | tf_op jit(solution)/shard_map/all_gather | solution.py:137
  217.9 4.1 %copy-start.4 = (f32[1024,256]{1,0:T(8,128)S(1)}, f32[1024,256]{1,0:T(8,128)}, u32[]{:S(2)}) copy-start(f32[1024,256]{1,0:T(8,128)} %copy-done.3) | copy-start | bytes 3145732
  222.0 28.1 %copy-start.10 = (f32[256]{0:T(256)S(1)}, f32[256]{0:T(256)}, u32[]{:S(2)}) copy-start(f32[256]{0:T(256)} %param.24) | copy-start | bytes 3076
  222.0 30.4 %copy-start.5 = (bf16[256,4096]{1,0:T(8,128)(2,1)S(1)}, bf16[256,4096]{1,0:T(8,128)(2,1)}, u32[]{:S(2)}) copy-start(bf16[256,4096]{1,0:T(8,128)(2,1)} %param.25) | copy-start | bytes 6291460
  254.9 94.7 %copy-start.6 = (bf16[1024,128]{1,0:T(8,128)(2,1)S(1)}, bf16[1024,128]{1,0:T(8,128)(2,1)}, u32[]{:S(2)}) copy-start(bf16[1024,128]{1,0:T(8,128)(2,1)} %param.14) | copy-start | bytes 786436
  349.7 11.8 %copy-start.1 = (bf16[4096,256]{1,0:T(8,128)(2,1)S(1)}, bf16[4096,256]{1,0:T(8,128)(2,1)}, u32[]{:S(2)}) copy-start(bf16[4096,256]{1,0:T(8,128)(2,1)} %param.17) | copy-start | bytes 6291460
Sparse Core Ops, SparseCore 0:
  24.2 105.6 all-gather.5
  168.7 37.5 all-gather.9
  252.6 97.0 all-gather.7
